TPU v7x, 32 devices: a whole 2x2x4 slice. The times are simulated.
32 devices in a mesh: groups: 2 (over x), tensor: 16 (over z, y, core).
Axes of the slice: x: 2, y: 2, z: 4, core: 2. Of those that a mesh axis runs over, the one named last changes fastest.
Arguments:
- tokens: bfloat16 [128, 4096], P(('groups', 'tensor')), parts along dimension 0, may hold values from -6 to 6
- expert_ids: int32 [128, 2], P(('groups', 'tensor')), parts along dimension 0, may hold values from 0 to 7, as said below
- gate_margin: float32 [128], P(('groups', 'tensor')), parts along dimension 0, may hold values from 0 to 2.5
- lengths: int32 [64], P('groups'), parts along dimension 0, may hold values from 1 to 8, 64 in all
- bench_ids: int32 [64], P('groups'), parts along dimension 0, may hold values from 0 to 7
- target: bfloat16 [128, 4096], P(('groups', 'tensor')), parts along dimension 0, may hold values from -3 to 3
- gate_up_weight: bfloat16 [16, 4096, 896], P('tensor'), may hold values from -0.09375 to 0.09375
- down_weight: bfloat16 [16, 448, 4096], P('tensor'), may hold values from -0.1875 to 0.1875
Outputs:
- mixed: bfloat16 [128, 4096], P(('groups', 'tensor')), parts along dimension 0
- load_ratio: float32 [16], P('groups'), parts along dimension 0
- bench_loss: float32 [16], P('groups'), parts along dimension 0
There are 2 independent parts, one for each index of `groups`. A program takes and returns all parts, laid end to end along the dimension named above; an argument that names none is the same for every part. Nothing has to cross between parts.
Inputs may be any that keep to these rules, and one draw needn't show every extreme that they name: `expert_ids`: each row names 2 different experts; every expert is named by some row; among the rows of one index of tensor no expert is named by more than 2 rows, and on the first and the last index of tensor some expert is named by exactly 2 rows. `lengths`: they sum to 64; the longest is exactly 8.
All inputs are finite; a program needn't handle non-finite values.
Results may differ from a plain program's by a relative error of at most 0.008.
Values may be sent and summed in bfloat16 or wider, within the bound.
A program may use at most 64 MiB of HBM per device.

v0:
```python
import jax
import jax.numpy as jnp
from jax import lax
from jax.sharding import PartitionSpec as P

EXPERTS = 8
TOP = 2
BENCH = 8


def expert_block(block_rows, gate_up_local, down_local):
    hidden = down_local.shape[0]
    gate_up_rows = jnp.dot(block_rows, gate_up_local, preferred_element_type=jnp.float32)
    activated = (jax.nn.silu(gate_up_rows[:, :hidden]) * gate_up_rows[:, hidden:]).astype(
        jnp.bfloat16
    )
    return jnp.dot(activated, down_local, preferred_element_type=jnp.float32).astype(jnp.bfloat16)


def slot_positions(flat_ids):
    onehot = (flat_ids[:, None] == jnp.arange(EXPERTS, dtype=jnp.int32)[None, :]).astype(jnp.int32)
    before = jnp.cumsum(onehot, axis=0) - onehot
    return (onehot, jnp.sum(before * onehot, axis=1))


def on_device(
    tokens, expert_ids, gate_margin, lengths, bench_ids, target, gate_up_weight, down_weight
):
    row_count = tokens.shape[0]
    model_width = tokens.shape[1]
    devices = lax.axis_size("tensor")
    group_size = devices // EXPERTS
    device_index = lax.axis_index("tensor")
    capacity = row_count * TOP // EXPERTS + 1
    gate_up_local = gate_up_weight[0]
    down_local = down_weight[0]
    flat_ids = expert_ids.reshape(-1)
    onehot, slot_index = slot_positions(flat_ids)
    local_load = jnp.sum(onehot, axis=0).astype(jnp.float32)
    global_load = lax.psum(local_load, "tensor")
    slot_range = jnp.arange(capacity, dtype=jnp.int32)
    pair_rows = jnp.repeat(tokens, TOP, axis=0)
    expert_range = jnp.arange(EXPERTS, dtype=jnp.int32)
    placement = (
        (flat_ids[None, None, :] == expert_range[:, None, None])
        & (slot_index[None, None, :] == slot_range[None, :, None])
    ).astype(jnp.bfloat16)
    outgoing = jnp.einsum(
        "ecp,pd->ecd", placement, pair_rows, preferred_element_type=jnp.float32
    ).astype(jnp.bfloat16)
    outgoing = jnp.repeat(outgoing, group_size, axis=0)
    received = lax.all_to_all(outgoing, "tensor", split_axis=0, concat_axis=0, tiled=True)
    source_count = received.shape[0]
    slot_count = received.shape[1]
    flat_rows = received.reshape(source_count * slot_count, model_width)
    partial_value = expert_block(flat_rows, gate_up_local, down_local).reshape(
        source_count, slot_count, model_width
    )
    returned = lax.all_to_all(partial_value, "tensor", split_axis=0, concat_axis=0, tiled=True)
    summed = jnp.sum(
        returned.reshape(EXPERTS, group_size, capacity, model_width).astype(jnp.float32), axis=1
    )
    picked = summed[flat_ids, slot_index].reshape(row_count, TOP, model_width)
    first_weight = jax.nn.sigmoid(gate_margin)[:, None]
    second_weight = jax.nn.sigmoid(-gate_margin)[:, None]
    mixed_exact = first_weight * picked[:, 0] + second_weight * picked[:, 1]
    mixed = mixed_exact.astype(jnp.bfloat16)
    token_loss = jnp.mean(jnp.square(mixed_exact - target.astype(jnp.float32)), axis=1)
    seq_ends = jnp.cumsum(lengths)
    positions = device_index * row_count + jnp.arange(row_count, dtype=jnp.int32)
    seq_hot = (
        (positions[:, None] >= (seq_ends - lengths)[None, :])
        & (positions[:, None] < seq_ends[None, :])
    ).astype(jnp.float32)
    bench_hot = (bench_ids[:, None] == jnp.arange(BENCH, dtype=jnp.int32)[None, :]).astype(
        jnp.float32
    )
    token_bench = jnp.dot(seq_hot, bench_hot, precision=lax.Precision.HIGHEST)
    local_loss = jnp.sum(token_loss[:, None] * token_bench, axis=0)
    global_loss = lax.psum(local_loss, "tensor")
    token_total = row_count * devices
    load_ratio = global_load * (EXPERTS / (TOP * token_total))
    bench_loss = global_loss / token_total
    return (mixed, load_ratio, bench_loss)


def solution(mesh):
    placed = (
        P(("groups", "tensor"), None),
        P(("groups", "tensor"), None),
        P(("groups", "tensor")),
        P("groups"),
        P("groups"),
        P(("groups", "tensor"), None),
        P("tensor", None, None),
        P("tensor", None, None),
    )
    return jax.shard_map(
        on_device,
        mesh=mesh,
        in_specs=placed,
        out_specs=(P(("groups", "tensor"), None), P("groups"), P("groups")),
        check_vma=False,
    )
```

profile of v0, /device:TPU:0, one launch (start us, length us, event | category | flops | bytes accessed | tf_op | source)
XLA Modules:
  0.0 74.7 jit_solution(5753095997943569445)
XLA Ops:
  0.6 0.8 %copy.23 = s32[4,2]{1,0:T(4,128)S(1)} copy(s32[4,2]{0,1:T(2,128)} %param.9) | data formatting | bytes 64 | tf_op args[1]
  1.4 0.1 eq.64
  1.5 0.1 iota_compare_fusion.3
  1.6 0.2 fusion.15
  1.8 0.8 %broadcast_in_dim.4 = bf16[4,2,4096]{2,1,0:T(2,128)(2,1)S(1)} broadcast(bf16[4,4096]{1,0:T(4,128)(2,1)} %param.8), dimensions={0,2} | broadcast | bytes 98304 | tf_op jit(solution)/shard_map/broadcast_in_dim | solution.py:42
  2.6 0.0 copy-start.2
  2.6 0.0 copy-start.3
  2.6 0.2 convolution_convert_fusion.1
  2.8 0.1 copy.24
  2.9 0.9 %broadcast_in_dim.5 = bf16[8,2,2,4096]{3,2,1,0:T(2,128)(2,1)} broadcast(bf16[8,2,4096]{2,1,0:T(2,128)(2,1)S(1)} %copy.24), dimensions={0,2,3} | broadcast | bytes 393216 | tf_op jit(solution)/shard_map/broadcast_in_dim | solution.py:51
  3.8 7.4 %all-to-all-start = ((bf16[16,2,4096]{2,1,0:T(2,128)(2,1)}), bf16[16,2,4096]{2,1,0:T(2,128)(2,1)S(1)}, u32[]{:S(2)}, u32[]{:S(2)}) async-start(bf16[16,2,4096]{2,1,0:T(2,128)(2,1)} %bitcast), calls=%async_computation | async-start | bytes 524288 | tf_op jit(solution)/shard_map/all_to_all | solution.py:52
  11.3 10.0 %all-to-all-done = bf16[16,2,4096]{2,1,0:T(2,128)(2,1)S(1)} async-done(((bf16[16,2,4096]{2,1,0:T(2,128)(2,1)}), bf16[16,2,4096]{2,1,0:T(2,128)(2,1)S(1)}, u32[]{:S(2)}, u32[]{:S(2)}) %all-to-all-start) | async-done | bytes 262176 | tf_op jit(solution)/shard_map/all_to_all | solution.py:52
  21.3 0.1 reshape.154
  21.4 0.0 copy-start
  21.4 0.0 copy-start.1
  21.4 0.0 copy-start.4
  21.4 4.4 %fusion = f32[32,896]{1,0:T(8,128)S(1)} fusion(bf16[32,4096]{1,0:T(8,128)(2,1)S(1)} %reshape.154, bf16[1,4096,896]{2,1,0:T(8,128)(2,1)} %param.14), kind=kOutput, calls=%fused_computation.1 | convolution fusion | flops 234881024 | bytes 7716864 | tf_op jit(solution)/shard_map/dot_general | solution.py:13
  25.9 0.0 copy-done
  25.9 0.8 %convolution_convert_fusion = bf16[32,4096]{1,0:T(8,128)(2,1)S(1)} fusion(bf16[1,448,4096]{2,1,0:T(8,128)(2,1)S(1)} %copy-done, f32[32,896]{1,0:T(8,128)S(1)} %fusion), kind=kOutput, calls=%fused_computation.3 | convolution fusion | flops 117657600 | bytes 4063232 | tf_op jit(solution)/shard_map/dot_general | solution.py:17
  26.7 0.9 %reshape.155 = bf16[16,2,4096]{2,1,0:T(2,128)(2,1)} reshape(bf16[32,4096]{1,0:T(8,128)(2,1)S(1)} %convolution_convert_fusion) | data formatting | bytes 524288 | tf_op jit(solution)/shard_map/reshape | solution.py:56
  27.6 3.5 %all-to-all-start.1 = ((bf16[16,2,4096]{2,1,0:T(2,128)(2,1)}), bf16[16,2,4096]{2,1,0:T(2,128)(2,1)S(1)}, u32[]{:S(2)}, u32[]{:S(2)}) async-start(bf16[16,2,4096]{2,1,0:T(2,128)(2,1)} %reshape.155), calls=%async_computation.1 | async-start | bytes 524288 | tf_op jit(solution)/shard_map/all_to_all | solution.py:59
  31.1 0.1 reshape.156
  31.2 0.0 copy-done.2
  31.2 0.1 copy.28
  31.3 0.1 reduce-window.8
  31.3 0.1 reduce
  31.5 0.0 copy-done.3
  31.5 9.6 %all-to-all-done.1 = bf16[16,2,4096]{2,1,0:T(2,128)(2,1)S(1)} async-done(((bf16[16,2,4096]{2,1,0:T(2,128)(2,1)}), bf16[16,2,4096]{2,1,0:T(2,128)(2,1)S(1)}, u32[]{:S(2)}, u32[]{:S(2)}) %all-to-all-start.1) | async-done | bytes 262176 | tf_op jit(solution)/shard_map/all_to_all | solution.py:59
  41.1 0.3 convert_reduce_fusion
  41.4 0.7 gather_fusion
  42.1 0.1 reshape.157
  42.2 0.1 fusion.30
  42.3 0.0 copy-done.1
  42.3 0.9 %multiply_reduce_fusion = (f32[4]{0:T(128)S(1)}, bf16[4,4096]{1,0:T(4,128)(2,1)}) fusion(bf16[4,4096]{1,0:T(4,128)(2,1)S(1)} %copy-done.1, f32[4,1,4096]{2,1,0:T(1,128)S(1)} %get-tuple-element.10, f32[4]{0:T(128)S(1)} %get-tuple-element.12, f32[4,1,4096]{2,1,0:T(1,128)S(1)} %get-tuple-element.9, f32[4]{0:T(128)S(1)} %get-tuple-element.11), kind=kLoop, calls=%fused_computation.16 | loop fusion | flops 131068 | bytes 196656 | tf_op jit(solution)/shard_map/reduce_sum | solution.py:68
  43.2 0.0 copy-done.4
  43.2 0.2 fusion.3
  43.4 30.8 %all-reduce = (f32[8]{0:T(128)S(1)}, f32[8]{0:T(128)S(1)}) all-reduce(f32[8]{0:T(128)S(1)} %convert_element_type.37, f32[8]{0:T(128)S(1)} %fusion.3), channel_id=1, replica_groups=mesh['groups'=2,'tensor'=16] {'tensor'}, use_global_device_ids=true, to_apply=%region_4.5 | all-reduce | flops 16 | bytes 128 | tf_op jit(solution)/shard_map/psum | solution.py:40
  74.2 0.5 broadcast_multiply_fusion
  (9 shorter events, 0.1 us)
Async XLA Ops:
  2.6 28.6 %copy-start.2 = (s32[32]{0:T(128)S(1)}, s32[32]{0:T(128)}, u32[]{:S(2)}) copy-start(s32[32]{0:T(128)} %param.11) | copy-start | bytes 388
  2.6 28.9 %copy-start.3 = (f32[4]{0:T(128)S(1)}, f32[4]{0:T(128)}, u32[]{:S(2)}) copy-start(f32[4]{0:T(128)} %param.10) | copy-start | bytes 52
  3.8 17.4 %all-to-all-start = ((bf16[16,2,4096]{2,1,0:T(2,128)(2,1)}), bf16[16,2,4096]{2,1,0:T(2,128)(2,1)S(1)}, u32[]{:S(2)}, u32[]{:S(2)}) async-start(bf16[16,2,4096]{2,1,0:T(2,128)(2,1)} %bitcast), calls=%async_computation | async-start | bytes 524288 | tf_op jit(solution)/shard_map/all_to_all | solution.py:52
  21.4 4.5 %copy-start = (bf16[1,448,4096]{2,1,0:T(8,128)(2,1)S(1)}, bf16[1,448,4096]{2,1,0:T(8,128)(2,1)}, u32[]{:S(2)}) copy-start(bf16[1,448,4096]{2,1,0:T(8,128)(2,1)} %param.15) | copy-start | bytes 11010052
  21.4 20.9 %copy-start.1 = (bf16[4,4096]{1,0:T(4,128)(2,1)S(1)}, bf16[4,4096]{1,0:T(4,128)(2,1)}, u32[]{:S(2)}) copy-start(bf16[4,4096]{1,0:T(4,128)(2,1)} %param.13) | copy-start | bytes 98308
  21.4 21.8 %copy-start.4 = (s32[32]{0:T(128)S(1)}, s32[32]{0:T(128)}, u32[]{:S(2)}) copy-start(s32[32]{0:T(128)} %param.12) | copy-start | bytes 388
  27.6 13.5 %all-to-all-start.1 = ((bf16[16,2,4096]{2,1,0:T(2,128)(2,1)}), bf16[16,2,4096]{2,1,0:T(2,128)(2,1)S(1)}, u32[]{:S(2)}, u32[]{:S(2)}) async-start(bf16[16,2,4096]{2,1,0:T(2,128)(2,1)} %reshape.155), calls=%async_computation.1 | async-start | bytes 524288 | tf_op jit(solution)/shard_map/all_to_all | solution.py:59
where the time goes:
time: 75.1 us; the launch traced here: 74.7 us
  blocking collectives  30.8 us (41%)
  waiting for transfers between devices  19.6 us (26%)
  starting transfers between devices  10.9 us (15%)
  matrix products  5.59 us (7%)
  local copies, waits for them, and re-layouts  4.83 us (6%)
  other arithmetic  2.19 us (3%)
  between operations  0.82 us (1%)
    psum x1, blocking collectives, on_device(): global_load = lax.psum(local_load, 'tensor')  30.8 us
    all_to_all x1, waiting for transfers between devices, on_device(): lax.all_to_all(outgoing, 'tensor', split_axis=0, concat_axis=0, tiled=True)  10 us
    all_to_all x1, waiting for transfers between devices, on_device(): lax.all_to_all(partial_value, 'tensor', split_axis=0, concat_axis=0, tile...  9.56 us
    all_to_all x1, starting transfers between devices, on_device(): lax.all_to_all(outgoing, 'tensor', split_axis=0, concat_axis=0, tiled=True)  7.41 us
    dot_general x1, matrix products, expert_block(): jnp.dot(block_rows, gate_up_local, preferred_element_type=jnp.float32)  4.42 us
    all_to_all x1, starting transfers between devices, on_device(): lax.all_to_all(partial_value, 'tensor', split_axis=0, concat_axis=0, tile...  3.53 us
  transfers between devices with their start and end apart: 2, of which 2 were waited for; matrix products, arithmetic and copies ran while one was open for 1% of the time, Pallas kernels for 0%

commit v1 on v0

v1 whole, which is shorter than its diff:
```python
import functools
import jax
import jax.numpy as jnp
from jax import lax
from jax.experimental import pallas as pl
from jax.experimental.pallas import tpu as pltpu
from jax.sharding import PartitionSpec as P

EXPERTS = 8
TOP = 2
BENCH = 8
F32 = jnp.float32
BF16 = jnp.bfloat16
I32 = jnp.int32


def iota(shape, dim):
    return lax.broadcasted_iota(I32, shape, dim)


def remote(src, dst, send_sem, recv_sem, device):
    return pltpu.make_async_remote_copy(
        src_ref=src,
        dst_ref=dst,
        send_sem=send_sem,
        recv_sem=recv_sem,
        device_id={"tensor": device},
        device_id_type=pl.DeviceIdType.MESH,
    )


def kernel(
    n,
    cap,
    tok_hbm,
    ids_hbm,
    margin_hbm,
    len_hbm,
    bench_hbm,
    target_hbm,
    gu_hbm,
    down_hbm,
    mixed_hbm,
    sums_ref,
    tok,
    ids,
    margin,
    lens,
    bench,
    target,
    gu_w,
    down_w,
    out,
    xbuf,
    psend,
    precv,
    ret,
    rbuf,
    mixed,
    row_send,
    rows_recv,
    in_sem,
    tok_sem,
    w_sem,
    d_sem,
    sem_s,
    sem_r,
    out_sem,
):
    rows, width = tok.shape
    half = width // 2
    hid = down_w.shape[0]
    group = n // EXPERTS
    slots = EXPERTS * cap
    total = n * cap
    me = lax.axis_index("tensor")
    core = lax.rem(me, 2)
    other = 1 - core
    partner = me + 1 - 2 * core
    pair = lax.div(me, 2)
    my_expert = lax.div(me, group)

    tok_cp = pltpu.make_async_copy(tok_hbm, tok, tok_sem.at[0])
    ids_cp = pltpu.make_async_copy(ids_hbm, ids, tok_sem.at[1])
    ids_cp.start()
    tok_cp.start()
    barrier = pltpu.get_barrier_semaphore()

    def greet(i, carry):
        pl.semaphore_signal(
            barrier,
            inc=1,
            device_id={"tensor": lax.rem(me + i, n)},
            device_id_type=pl.DeviceIdType.MESH,
        )
        return carry

    lax.fori_loop(1, n, greet, 0)
    smalls = [
        pltpu.make_async_copy(a, b, in_sem.at[i])
        for i, (a, b) in enumerate(
            ((margin_hbm, margin), (len_hbm, lens), (bench_hbm, bench), (target_hbm, target))
        )
    ]
    for cp in smalls:
        cp.start()
    own_rows = pl.ds(pl.multiple_of(core * half, half), half)
    other_rows = pl.ds(pl.multiple_of(other * half, half), half)
    w_own = pltpu.make_async_copy(gu_hbm.at[0, own_rows], gu_w.at[own_rows], w_sem.at[0])
    w_other = pltpu.make_async_copy(gu_hbm.at[0, other_rows], gu_w.at[other_rows], w_sem.at[1])
    w_down = pltpu.make_async_copy(down_hbm.at[0], down_w, w_sem.at[2])
    w_own.start()
    w_other.start()
    w_down.start()

    ids_cp.wait()
    tok_cp.wait()
    id_rows = ids[...]
    slot_row = iota((slots, 1), 0)
    slot_expert = slot_row // cap
    slot_place = slot_row - slot_expert * cap
    seen = jnp.zeros((slots, 1), I32)
    packed = jnp.zeros((slots, width), F32)
    for t in range(rows):
        hit = (id_rows[t : t + 1, 0:1] == slot_expert) | (id_rows[t : t + 1, 1:2] == slot_expert)
        chosen = jnp.where(hit & (seen == slot_place), 1.0, 0.0).astype(F32)
        packed = packed + chosen * tok[t : t + 1, :].astype(F32)
        seen = seen + jnp.where(hit, 1, 0)
    packed = packed.astype(BF16)
    for e in range(EXPERTS):
        for h in range(2):
            out[h, e] = packed[e * cap : (e + 1) * cap, h * half : (h + 1) * half]
    xbuf[core, me] = out[core, my_expert]

    pl.semaphore_wait(barrier, n - 1)

    def dispatch(i, carry):
        d = lax.rem(me + i, n)
        h = lax.rem(d, 2)
        remote(
            out.at[h, lax.div(d, group)], xbuf.at[h, me], sem_s.at[0], sem_r.at[0], d
        ).start()
        return carry

    lax.fori_loop(1, n, dispatch, 0)

    for cp in smalls:
        cp.wait()
    seqs = lens.shape[1]
    across = iota((seqs, seqs), 1)
    down_axis = iota((seqs, seqs), 0)
    len_row = lens[...]
    len_col = jnp.sum(jnp.where(across == down_axis, len_row, 0).astype(F32), axis=1, keepdims=True)
    ends = jnp.sum(jnp.where(down_axis <= across, len_col, 0.0), axis=0, keepdims=True)
    starts = ends - len_row.astype(F32)
    position = (me * rows + iota((rows, seqs), 0)).astype(F32)
    in_seq = (position >= starts) & (position < ends)
    token_bench = (
        jnp.sum(
            jnp.where(in_seq, bench[...].astype(F32) + 1.0, 0.0), axis=1, keepdims=True
        )
        - 1.0
    )
    lane = iota((rows, 128), 1)
    bench_hot = jnp.where(token_bench == lane.astype(F32), 1.0, 0.0)
    load_hot = jnp.where(
        (id_rows[:, 0:1] + BENCH == lane) | (id_rows[:, 1:2] + BENCH == lane), 1.0, 0.0
    )

    terms = 32
    pairs_rows = total // 2
    col = iota((1, pairs_rows), 1)
    col_expert = (col // cap) // (group // 2)
    col_place = lax.rem(col, cap)
    term_row = iota((terms, pairs_rows), 0)
    weights = jnp.zeros((terms, pairs_rows), F32)
    seen = jnp.zeros((1, pairs_rows), I32)
    for t in range(rows):
        first = id_rows[t : t + 1, 0:1] == col_expert
        second = id_rows[t : t + 1, 1:2] == col_expert
        m = margin[0:1, t : t + 1]
        gate = jnp.where(first, 1.0 / (1.0 + jnp.exp(-m)), 0.0) + jnp.where(
            second, 1.0 / (1.0 + jnp.exp(m)), 0.0
        )
        gate = jnp.where(seen == col_place, gate, 0.0)
        weights = weights + jnp.where(lax.rem(term_row, 8) == t, gate, 0.0)
        seen = seen + jnp.where(first | second, 1, 0)
    high = weights.astype(BF16).astype(F32)
    mid = (weights - high).astype(BF16).astype(F32)
    low = weights - high - mid
    weights = jnp.where(
        term_row < 8,
        high,
        jnp.where(term_row < 16, mid, jnp.where(term_row < 24, low, 0.0)),
    ).astype(BF16)

    remote(xbuf.at[core, pl.ds(0, n - 1)], xbuf.at[core, pl.ds(0, n - 1)], sem_s.at[0], sem_r.at[0], partner).wait_recv()
    forward = remote(xbuf.at[core], xbuf.at[core], sem_s.at[1], sem_r.at[1], partner)
    forward.start()
    w_own.wait()
    x = jnp.concatenate([xbuf[core, i] for i in range(n)], axis=0)
    both = jnp.dot(x, gu_w[own_rows, :], preferred_element_type=F32)
    w_other.wait()
    forward.wait_recv()
    x = jnp.concatenate([xbuf[other, i] for i in range(n)], axis=0)
    both = both + jnp.dot(x, gu_w[other_rows, :], preferred_element_type=F32)
    v = both[:, :hid]
    act = (v / (1.0 + jnp.exp(-v)) * both[:, hid:]).astype(BF16)
    w_down.wait()

    pieces = psend.shape[0]
    piece = half // pieces
    swaps = []
    for j in range(pieces):
        columns = pl.ds(pl.multiple_of(other * half + j * piece, piece), piece)
        psend[j] = jnp.dot(act, down_w[:, columns], preferred_element_type=F32).astype(BF16)
        swap = remote(psend.at[j], precv.at[j], d_sem.at[0, j], d_sem.at[1, j], partner)
        swap.start()
        swaps.append(swap)
    for j in range(pieces):
        columns = pl.ds(pl.multiple_of(core * half + j * piece, piece), piece)
        mine = jnp.dot(act, down_w[:, columns], preferred_element_type=F32)
        swaps[j].wait_recv()
        summed = (mine + precv[j].astype(F32)).astype(BF16)
        for i in range(n):
            ret[i, :, j * piece : (j + 1) * piece] = summed[i * cap : (i + 1) * cap, :]

    def give_back(i, carry):
        d = lax.rem(me + i, n)
        remote(ret.at[d], rbuf.at[core, pair], sem_s.at[2], sem_r.at[2], d).start()
        return carry

    lax.fori_loop(1, n, give_back, 0)
    rbuf[core, pair] = ret[me]
    stand_in = xbuf.at[0, pl.ds(0, n - 1)]
    remote(stand_in, stand_in, sem_s.at[2], sem_r.at[2], partner).wait_recv()

    loss = jnp.zeros((rows, 1), F32)
    for h in range(2):
        got = jnp.concatenate([rbuf[h, i] for i in range(n // 2)], axis=0)
        parts = jnp.dot(weights, got, preferred_element_type=F32)
        exact = (parts[0:8] + parts[8:16] + parts[16:24])[:rows]
        span = slice(h * half, (h + 1) * half)
        mixed[:, span] = exact.astype(BF16)
        gap = exact - target[:, span].astype(F32)
        loss = loss + jnp.sum(gap * gap, axis=1, keepdims=True)
    loss = loss * (1.0 / width)
    mine = jnp.sum(bench_hot * loss + load_hot, axis=0, keepdims=True)
    row_send[0] = mine
    rows_recv[me] = mine

    def share(i, carry):
        remote(
            row_send.at[0], rows_recv.at[me], sem_s.at[3], sem_r.at[3], lax.rem(me + i, n)
        ).start()
        return carry

    lax.fori_loop(1, n, share, 0)
    mixed_cp = pltpu.make_async_copy(mixed, mixed_hbm, out_sem)
    mixed_cp.start()
    remote(stand_in, stand_in, sem_s.at[0], sem_r.at[0], partner).wait_send()
    forward.wait_send()
    for swap in swaps:
        swap.wait_send()
    remote(stand_in, stand_in, sem_s.at[2], sem_r.at[2], partner).wait_send()
    all_rows = rows_recv.at[pl.ds(0, n - 1)]
    shared = remote(all_rows, all_rows, sem_s.at[3], sem_r.at[3], partner)
    shared.wait_recv()
    everyone = jnp.sum(rows_recv[...], axis=0)
    token_total = rows * n
    lane = iota((1, 128), 1)
    sums_ref[...] = everyone * jnp.where(
        lane < BENCH, 1.0 / token_total, EXPERTS / (TOP * token_total)
    )
    shared.wait_send()
    mixed_cp.wait()


def on_device(
    tokens, expert_ids, gate_margin, lengths, bench_ids, target, gate_up_weight, down_weight
):
    n = lax.axis_size("tensor")
    rows, width = tokens.shape
    cap = rows * TOP // EXPERTS + 1
    half = width // 2
    hid = down_weight.shape[1]
    pieces = 2
    seqs = lengths.shape[0]
    hbm = pl.BlockSpec(memory_space=pl.ANY)
    mixed, sums = pl.pallas_call(
        functools.partial(kernel, n, cap),
        out_shape=(
            jax.ShapeDtypeStruct((rows, width), BF16),
            jax.ShapeDtypeStruct((1, 128), F32),
        ),
        in_specs=[hbm] * 8,
        out_specs=(hbm, pl.BlockSpec(memory_space=pltpu.VMEM)),
        scratch_shapes=[
            pltpu.VMEM((rows, width), BF16),
            pltpu.VMEM((rows, TOP), I32),
            pltpu.VMEM((1, rows), F32),
            pltpu.VMEM((1, seqs), I32),
            pltpu.VMEM((1, seqs), I32),
            pltpu.VMEM((rows, width), BF16),
            pltpu.VMEM((width, 2 * hid), BF16),
            pltpu.VMEM((hid, width), BF16),
            pltpu.VMEM((2, EXPERTS, cap, half), BF16),
            pltpu.VMEM((2, n, cap, half), BF16),
            pltpu.VMEM((pieces, n * cap, half // pieces), BF16),
            pltpu.VMEM((pieces, n * cap, half // pieces), BF16),
            pltpu.VMEM((n, cap, half), BF16),
            pltpu.VMEM((2, n // 2, cap, half), BF16),
            pltpu.VMEM((rows, width), BF16),
            pltpu.VMEM((1, 1, 128), F32),
            pltpu.VMEM((n, 1, 128), F32),
            pltpu.SemaphoreType.DMA((4,)),
            pltpu.SemaphoreType.DMA((2,)),
            pltpu.SemaphoreType.DMA((3,)),
            pltpu.SemaphoreType.DMA((2, pieces)),
            pltpu.SemaphoreType.DMA((4,)),
            pltpu.SemaphoreType.DMA((4,)),
            pltpu.SemaphoreType.DMA,
        ],
        compiler_params=pltpu.CompilerParams(
            collective_id=0, has_side_effects=True, vmem_limit_bytes=60 * 1024 * 1024
        ),
    )(
        tokens,
        expert_ids,
        gate_margin.reshape(1, rows),
        lengths.reshape(1, seqs),
        bench_ids.reshape(1, seqs),
        target,
        gate_up_weight,
        down_weight,
    )
    return mixed, sums[0, BENCH : BENCH + EXPERTS], sums[0, :BENCH]


def solution(mesh):
    placed = (
        P(("groups", "tensor"), None),
        P(("groups", "tensor"), None),
        P(("groups", "tensor")),
        P("groups"),
        P("groups"),
        P(("groups", "tensor"), None),
        P("tensor", None, None),
        P("tensor", None, None),
    )
    return jax.shard_map(
        on_device,
        mesh=mesh,
        in_specs=placed,
        out_specs=(P(("groups", "tensor"), None), P("groups"), P("groups")),
        check_vma=False,
    )
```

time: 75.1 us -> 29.8 us (0.40)
  blocking collectives: 30.8 us -> 0 us
  Pallas kernels: 0 us -> 24.9 us
  waiting for transfers between devices: 19.6 us -> 0 us
  starting transfers between devices: 10.9 us -> 0 us
  matrix products: 5.59 us -> 0 us
  other arithmetic: 2.19 us -> 0 us
  local copies, waits for them, and re-layouts: 4.83 us -> 4.01 us
    psum x1 -> x0, blocking collectives: 30.8 us -> none  [on_device(): global_load = lax.psum(local_load, 'tensor')]
    pallas_call x0 -> x1, Pallas kernels: none -> 24.9 us  [on_device(): pl.pallas_call(functools.partial(kernel, n, cap), out_shape=(jax.ShapeDty...]
    all_to_all x2 -> x0, waiting for transfers between devices: 19.6 us -> none  [the longest x1 10 us: on_device(): lax.all_to_all(outgoing, 'tensor', split_axis=0, concat_axis=0, tiled=True)]
    all_to_all x2 -> x0, starting transfers between devices: 10.9 us -> none  [the longest x1 7.41 us: on_device(): lax.all_to_all(outgoing, 'tensor', split_axis=0, concat_axis=0, tiled=True)]
    dot_general x4 -> x0, matrix products: 5.59 us -> none  [the longest x1 4.42 us: expert_block(): jnp.dot(block_rows, gate_up_local, preferred_element_type=jnp.float32)]
    unnamed x11 -> x2, local copies, waits for them, and re-layouts: 0.8 us -> 2.72 us
    broadcast_in_dim x2 -> x0, local copies, waits for them, and re-layouts: 1.69 us -> none  [the longest x1 0.9 us: on_device(): outgoing = jnp.repeat(outgoing, group_size, axis=0)]
    reduce_sum x3 -> x0, other arithmetic: 1.34 us -> none  [the longest x1 0.85 us: on_device(): jnp.mean(jnp.square(mixed_exact - target.astype(jnp.float32)), axis=1)]
  transfers between devices with their start and end apart: 2 -> 0, of which waited for: 2 -> 0; matrix products, arithmetic and copies ran while one was open for 1% -> 0% of each run, Pallas kernels for 0% -> 0%
where the time goes in v1:
time: 29.8 us; the launch traced here: 29.6 us
  Pallas kernels  24.9 us (84%)
  local copies, waits for them, and re-layouts  4.01 us (13%)
  between operations  0.64 us (2%)
    pallas_call x1, Pallas kernels, on_device(): pl.pallas_call(functools.partial(kernel, n, cap), out_shape=(jax.ShapeDty...  24.9 us
    unnamed x2, local copies, waits for them, and re-layouts  2.72 us
    squeeze x1, local copies, waits for them, and re-layouts, on_device(): return (mixed, sums[0, BENCH:BENCH + EXPERTS], sums[0, :BENCH])  1.29 us

profile of v1, /device:TPU:0, one launch (start us, length us, event | category | flops | bytes accessed | tf_op | source)
XLA Modules:
  0.0 29.6 jit_solution(14237382917650283030)
XLA Ops:
  0.6 1.3 %copy.11.ids_hbm = s32[4,2]{1,0:T(4,128)} copy(s32[4,2]{0,1:T(2,128)} %param.9) | data formatting | bytes 64 | tf_op args[1]
  2.0 24.9 %shard_map.103 = (bf16[4,4096]{1,0:T(4,128)(2,1)}, f32[1,128]{1,0:T(1,128)}) custom-call(bf16[4,4096]{1,0:T(4,128)(2,1)} %tok_hbm.1, s32[4,2]{1,0:T(4,128)} %copy.11.ids_hbm, f32[1,4]{1,0:T(1,128)} %bitcast.7, s32[1,32]{1,0:T(1,128)} %bitcast.8, s32[1,32]{1,0:T(1,128)} %bitcast.9, bf16[4,4096]{1,0:T(4,128)(2,1)} %target_hbm.1, bf16[1,4096,896]{2,1,0:T(8,128)(2,1)} %gu_hbm.1, ...), custom_call_target="tpu_custom_call" | custom-call | tf_op jit(solution)/shard_map/pallas_call | solution.py:290
  26.9 1.3 %slice_bitcast_fusion = (f32[8]{0:T(128)}, f32[8]{0:T(128)}) fusion(f32[1,128]{1,0:T(1,128)} %get-tuple-element.6), kind=kLoop, calls=%fused_computation | loop fusion | bytes 128 | tf_op jit(solution)/shard_map/squeeze | solution.py:337
  28.2 1.4 %copy.13 = bf16[4,4096]{1,0:T(4,128)(2,1)} copy(bf16[4,4096]{1,0:T(4,128)(2,1)} %get-tuple-element.12) | data formatting | bytes 65536

commit v2 on v1

--- a/solution.py
+++ b/solution.py
@@ -80,22 +80,27 @@
     pair = lax.div(me, 2)
     my_expert = lax.div(me, group)
 
+    flips = [
+        (1 - 2 * lax.rem(lax.div(me, 1 << b), 2)) * (1 << b) for b in range((n - 1).bit_length())
+    ]
+    peers = []
+    for i in range(n - 1, 0, -1):
+        d = me
+        for b, flip in enumerate(flips):
+            if (i >> b) & 1:
+                d = d + flip
+        peers.append(d)
+
     tok_cp = pltpu.make_async_copy(tok_hbm, tok, tok_sem.at[0])
     ids_cp = pltpu.make_async_copy(ids_hbm, ids, tok_sem.at[1])
     ids_cp.start()
     tok_cp.start()
     barrier = pltpu.get_barrier_semaphore()
 
-    def greet(i, carry):
+    for d in peers:
         pl.semaphore_signal(
-            barrier,
-            inc=1,
-            device_id={"tensor": lax.rem(me + i, n)},
-            device_id_type=pl.DeviceIdType.MESH,
+            barrier, inc=1, device_id={"tensor": d}, device_id_type=pl.DeviceIdType.MESH
         )
-        return carry
-
-    lax.fori_loop(1, n, greet, 0)
     smalls = [
         pltpu.make_async_copy(a, b, in_sem.at[i])
         for i, (a, b) in enumerate(
@@ -122,7 +127,7 @@
     seen = jnp.zeros((slots, 1), I32)
     packed = jnp.zeros((slots, width), F32)
     for t in range(rows):
-        hit = (id_rows[t : t + 1, 0:1] == slot_expert) | (id_rows[t : t + 1, 1:2] == slot_expert)
+        hit = (id_rows[0:1, t : t + 1] == slot_expert) | (id_rows[1:2, t : t + 1] == slot_expert)
         chosen = jnp.where(hit & (seen == slot_place), 1.0, 0.0).astype(F32)
         packed = packed + chosen * tok[t : t + 1, :].astype(F32)
         seen = seen + jnp.where(hit, 1, 0)
@@ -134,15 +139,11 @@
 
     pl.semaphore_wait(barrier, n - 1)
 
-    def dispatch(i, carry):
-        d = lax.rem(me + i, n)
+    for d in peers:
         h = lax.rem(d, 2)
         remote(
             out.at[h, lax.div(d, group)], xbuf.at[h, me], sem_s.at[0], sem_r.at[0], d
         ).start()
-        return carry
-
-    lax.fori_loop(1, n, dispatch, 0)
 
     for cp in smalls:
         cp.wait()
@@ -163,9 +164,10 @@
     )
     lane = iota((rows, 128), 1)
     bench_hot = jnp.where(token_bench == lane.astype(F32), 1.0, 0.0)
-    load_hot = jnp.where(
-        (id_rows[:, 0:1] + BENCH == lane) | (id_rows[:, 1:2] + BENCH == lane), 1.0, 0.0
-    )
+    load_hot = jnp.zeros((1, 128), F32)
+    for t in range(rows):
+        for k in range(TOP):
+            load_hot = load_hot + jnp.where(id_rows[k : k + 1, t : t + 1] + BENCH == lane[0:1], 1.0, 0.0)
 
     terms = 32
     pairs_rows = total // 2
@@ -176,8 +178,8 @@
     weights = jnp.zeros((terms, pairs_rows), F32)
     seen = jnp.zeros((1, pairs_rows), I32)
     for t in range(rows):
-        first = id_rows[t : t + 1, 0:1] == col_expert
-        second = id_rows[t : t + 1, 1:2] == col_expert
+        first = id_rows[0:1, t : t + 1] == col_expert
+        second = id_rows[1:2, t : t + 1] == col_expert
         m = margin[0:1, t : t + 1]
         gate = jnp.where(first, 1.0 / (1.0 + jnp.exp(-m)), 0.0) + jnp.where(
             second, 1.0 / (1.0 + jnp.exp(m)), 0.0
@@ -223,46 +225,45 @@
         swaps[j].wait_recv()
         summed = (mine + precv[j].astype(F32)).astype(BF16)
         for i in range(n):
-            ret[i, :, j * piece : (j + 1) * piece] = summed[i * cap : (i + 1) * cap, :]
-
-    def give_back(i, carry):
-        d = lax.rem(me + i, n)
-        remote(ret.at[d], rbuf.at[core, pair], sem_s.at[2], sem_r.at[2], d).start()
-        return carry
-
-    lax.fori_loop(1, n, give_back, 0)
-    rbuf[core, pair] = ret[me]
+            ret[j, i] = summed[i * cap : (i + 1) * cap, :]
+        for d in peers:
+            remote(
+                ret.at[j, d], rbuf.at[core, j, pair], d_sem.at[2, j], d_sem.at[3, j], d
+            ).start()
+        rbuf[core, j, pair] = ret[j, me]
+
     stand_in = xbuf.at[0, pl.ds(0, n - 1)]
-    remote(stand_in, stand_in, sem_s.at[2], sem_r.at[2], partner).wait_recv()
+    returned = []
+    for j in range(pieces):
+        sent = ret.at[j, pl.ds(0, n - 1)]
+        returned.append(remote(sent, sent, d_sem.at[2, j], d_sem.at[3, j], partner))
 
     loss = jnp.zeros((rows, 1), F32)
-    for h in range(2):
-        got = jnp.concatenate([rbuf[h, i] for i in range(n // 2)], axis=0)
-        parts = jnp.dot(weights, got, preferred_element_type=F32)
-        exact = (parts[0:8] + parts[8:16] + parts[16:24])[:rows]
-        span = slice(h * half, (h + 1) * half)
-        mixed[:, span] = exact.astype(BF16)
-        gap = exact - target[:, span].astype(F32)
-        loss = loss + jnp.sum(gap * gap, axis=1, keepdims=True)
+    for j in range(pieces):
+        returned[j].wait_recv()
+        for h in range(2):
+            got = jnp.concatenate([rbuf[h, j, i] for i in range(n // 2)], axis=0)
+            parts = jnp.dot(weights, got, preferred_element_type=F32)
+            exact = (parts[0:8] + parts[8:16] + parts[16:24])[:rows]
+            span = slice(h * half + j * piece, h * half + (j + 1) * piece)
+            mixed[:, span] = exact.astype(BF16)
+            gap = exact - target[:, span].astype(F32)
+            loss = loss + jnp.sum(gap * gap, axis=1, keepdims=True)
     loss = loss * (1.0 / width)
-    mine = jnp.sum(bench_hot * loss + load_hot, axis=0, keepdims=True)
+    mine = jnp.sum(bench_hot * loss, axis=0, keepdims=True) + load_hot
     row_send[0] = mine
     rows_recv[me] = mine
 
-    def share(i, carry):
-        remote(
-            row_send.at[0], rows_recv.at[me], sem_s.at[3], sem_r.at[3], lax.rem(me + i, n)
-        ).start()
-        return carry
-
-    lax.fori_loop(1, n, share, 0)
+    for d in peers:
+        remote(row_send.at[0], rows_recv.at[me], sem_s.at[3], sem_r.at[3], d).start()
     mixed_cp = pltpu.make_async_copy(mixed, mixed_hbm, out_sem)
     mixed_cp.start()
     remote(stand_in, stand_in, sem_s.at[0], sem_r.at[0], partner).wait_send()
     forward.wait_send()
     for swap in swaps:
         swap.wait_send()
-    remote(stand_in, stand_in, sem_s.at[2], sem_r.at[2], partner).wait_send()
+    for back in returned:
+        back.wait_send()
     all_rows = rows_recv.at[pl.ds(0, n - 1)]
     shared = remote(all_rows, all_rows, sem_s.at[3], sem_r.at[3], partner)
     shared.wait_recv()
@@ -274,6 +275,13 @@
     )
     shared.wait_send()
     mixed_cp.wait()
+
+
+def finish(mixed_in, sums_in, mixed_ref, load_ref, loss_ref):
+    mixed_ref[...] = mixed_in[...]
+    sums = sums_in[...]
+    load_ref[...] = sums[:, BENCH : BENCH + EXPERTS]
+    loss_ref[...] = sums[:, :BENCH]
 
 
 def on_device(
@@ -297,7 +305,7 @@
         out_specs=(hbm, pl.BlockSpec(memory_space=pltpu.VMEM)),
         scratch_shapes=[
             pltpu.VMEM((rows, width), BF16),
-            pltpu.VMEM((rows, TOP), I32),
+            pltpu.VMEM((TOP, rows), I32),
             pltpu.VMEM((1, rows), F32),
             pltpu.VMEM((1, seqs), I32),
             pltpu.VMEM((1, seqs), I32),
@@ -308,15 +316,15 @@
             pltpu.VMEM((2, n, cap, half), BF16),
             pltpu.VMEM((pieces, n * cap, half // pieces), BF16),
             pltpu.VMEM((pieces, n * cap, half // pieces), BF16),
-            pltpu.VMEM((n, cap, half), BF16),
-            pltpu.VMEM((2, n // 2, cap, half), BF16),
+            pltpu.VMEM((pieces, n, cap, half // pieces), BF16),
+            pltpu.VMEM((2, pieces, n // 2, cap, half // pieces), BF16),
             pltpu.VMEM((rows, width), BF16),
             pltpu.VMEM((1, 1, 128), F32),
             pltpu.VMEM((n, 1, 128), F32),
             pltpu.SemaphoreType.DMA((4,)),
             pltpu.SemaphoreType.DMA((2,)),
             pltpu.SemaphoreType.DMA((3,)),
-            pltpu.SemaphoreType.DMA((2, pieces)),
+            pltpu.SemaphoreType.DMA((4, pieces)),
             pltpu.SemaphoreType.DMA((4,)),
             pltpu.SemaphoreType.DMA((4,)),
             pltpu.SemaphoreType.DMA,
@@ -326,7 +334,7 @@
         ),
     )(
         tokens,
-        expert_ids,
+        expert_ids.T,
         gate_margin.reshape(1, rows),
         lengths.reshape(1, seqs),
         bench_ids.reshape(1, seqs),
@@ -334,7 +342,18 @@
         gate_up_weight,
         down_weight,
     )
-    return mixed, sums[0, BENCH : BENCH + EXPERTS], sums[0, :BENCH]
+    vmem = pl.BlockSpec(memory_space=pltpu.VMEM)
+    mixed, load, bench_loss = pl.pallas_call(
+        finish,
+        out_shape=(
+            jax.ShapeDtypeStruct((rows, width), BF16),
+            jax.ShapeDtypeStruct((1, EXPERTS), F32),
+            jax.ShapeDtypeStruct((1, BENCH), F32),
+        ),
+        in_specs=[vmem, vmem],
+        out_specs=(vmem, vmem, vmem),
+    )(mixed, sums)
+    return mixed, load.reshape(EXPERTS), bench_loss.reshape(BENCH)
 
 
 def solution(mesh):

time: 29.8 us -> 27.1 us (0.909)
  local copies, waits for them, and re-layouts: 4.01 us -> 0 us
  Pallas kernels: 24.9 us -> 26.2 us
    unnamed x2 -> x0, local copies, waits for them, and re-layouts: 2.72 us -> none
    pallas_call x0 -> x1, Pallas kernels: none -> 1.38 us  [on_device(): pl.pallas_call(finish, out_shape=(jax.ShapeDtypeStruct((rows, width), BF1...]
    squeeze x1 -> x0, local copies, waits for them, and re-layouts: 1.29 us -> none  [on_device(): return (mixed, sums[0, BENCH:BENCH + EXPERTS], sums[0, :BENCH])]
where the time goes in v2:
time: 27.1 us; the launch traced here: 26.9 us
  Pallas kernels  26.2 us (97%)
  between operations  0.64 us (2%)
    pallas_call x1, Pallas kernels, on_device(): pl.pallas_call(functools.partial(kernel, n, cap), out_shape=(jax.ShapeDty...  24.8 us
    pallas_call x1, Pallas kernels, on_device(): pl.pallas_call(finish, out_shape=(jax.ShapeDtypeStruct((rows, width), BF1...  1.38 us

profile of v2, /device:TPU:0, one launch (start us, length us, event | category | flops | bytes accessed | tf_op | source)
XLA Modules:
  0.0 26.9 jit_solution(18399009814979428617)
XLA Ops:
  0.6 24.8 %shard_map.103 = (bf16[4,4096]{1,0:T(4,128)(2,1)}, f32[1,128]{1,0:T(1,128)}) custom-call(bf16[4,4096]{1,0:T(4,128)(2,1)} %tok_hbm.1, s32[2,4]{1,0:T(2,128)} %bitcast.6, f32[1,4]{1,0:T(1,128)} %bitcast.7, s32[1,32]{1,0:T(1,128)} %bitcast.8, s32[1,32]{1,0:T(1,128)} %bitcast.9, bf16[4,4096]{1,0:T(4,128)(2,1)} %target_hbm.1, bf16[1,4096,896]{2,1,0:T(8,128)(2,1)} %gu_hbm.1, ...), custom_call_target="tpu_custom_call" | custom-call | tf_op jit(solution)/shard_map/pallas_call | solution.py:298
  25.5 1.4 %shard_map.104 = (bf16[4,4096]{1,0:T(4,128)(2,1)}, f32[1,8]{1,0:T(1,128)}, f32[1,8]{1,0:T(1,128)}) custom-call(bf16[4,4096]{1,0:T(4,128)(2,1)} %get-tuple-element.8.mixed_in, f32[1,128]{1,0:T(1,128)} %get-tuple-element.9.sums_in), custom_call_target="tpu_custom_call" | custom-call | tf_op jit(solution)/shard_map/pallas_call | solution.py:346

commit v3 on v2

--- a/solution.py
+++ b/solution.py
@@ -40,7 +40,7 @@
     target_hbm,
     gu_hbm,
     down_hbm,
-    mixed_hbm,
+    mixed,
     sums_ref,
     tok,
     ids,
@@ -52,11 +52,11 @@
     down_w,
     out,
     xbuf,
-    psend,
-    precv,
+    down_p,
+    act_send,
+    act_recv,
     ret,
     rbuf,
-    mixed,
     row_send,
     rows_recv,
     in_sem,
@@ -65,7 +65,6 @@
     d_sem,
     sem_s,
     sem_r,
-    out_sem,
 ):
     rows, width = tok.shape
     half = width // 2
@@ -113,7 +112,9 @@
     other_rows = pl.ds(pl.multiple_of(other * half, half), half)
     w_own = pltpu.make_async_copy(gu_hbm.at[0, own_rows], gu_w.at[own_rows], w_sem.at[0])
     w_other = pltpu.make_async_copy(gu_hbm.at[0, other_rows], gu_w.at[other_rows], w_sem.at[1])
-    w_down = pltpu.make_async_copy(down_hbm.at[0], down_w, w_sem.at[2])
+    own_cols = pl.ds(pl.multiple_of(core * half, half), half)
+    other_cols = pl.ds(pl.multiple_of(other * half, half), half)
+    w_down = pltpu.make_async_copy(down_hbm.at[0, :, own_cols], down_w, w_sem.at[2])
     w_own.start()
     w_other.start()
     w_down.start()
@@ -144,6 +145,8 @@
         remote(
             out.at[h, lax.div(d, group)], xbuf.at[h, me], sem_s.at[0], sem_r.at[0], d
         ).start()
+    lend = remote(down_hbm.at[0, :, other_cols], down_p, sem_s.at[2], sem_r.at[2], partner)
+    lend.start()
 
     for cp in smalls:
         cp.wait()
@@ -210,20 +213,21 @@
     act = (v / (1.0 + jnp.exp(-v)) * both[:, hid:]).astype(BF16)
     w_down.wait()
 
-    pieces = psend.shape[0]
+    act_send[...] = act
+    swap = remote(act_send, act_recv, sem_s.at[4], sem_r.at[4], partner)
+    swap.start()
+    pieces = ret.shape[0]
     piece = half // pieces
-    swaps = []
+    mine = [
+        jnp.dot(act, down_w[:, j * piece : (j + 1) * piece], preferred_element_type=F32)
+        for j in range(pieces)
+    ]
+    swap.wait_recv()
+    lend.wait_recv()
+    act = act_recv[...]
     for j in range(pieces):
-        columns = pl.ds(pl.multiple_of(other * half + j * piece, piece), piece)
-        psend[j] = jnp.dot(act, down_w[:, columns], preferred_element_type=F32).astype(BF16)
-        swap = remote(psend.at[j], precv.at[j], d_sem.at[0, j], d_sem.at[1, j], partner)
-        swap.start()
-        swaps.append(swap)
-    for j in range(pieces):
-        columns = pl.ds(pl.multiple_of(core * half + j * piece, piece), piece)
-        mine = jnp.dot(act, down_w[:, columns], preferred_element_type=F32)
-        swaps[j].wait_recv()
-        summed = (mine + precv[j].astype(F32)).astype(BF16)
+        theirs = jnp.dot(act, down_p[:, j * piece : (j + 1) * piece], preferred_element_type=F32)
+        summed = (mine[j] + theirs).astype(BF16)
         for i in range(n):
             ret[j, i] = summed[i * cap : (i + 1) * cap, :]
         for d in peers:
@@ -256,12 +260,10 @@
 
     for d in peers:
         remote(row_send.at[0], rows_recv.at[me], sem_s.at[3], sem_r.at[3], d).start()
-    mixed_cp = pltpu.make_async_copy(mixed, mixed_hbm, out_sem)
-    mixed_cp.start()
     remote(stand_in, stand_in, sem_s.at[0], sem_r.at[0], partner).wait_send()
     forward.wait_send()
-    for swap in swaps:
-        swap.wait_send()
+    swap.wait_send()
+    lend.wait_send()
     for back in returned:
         back.wait_send()
     all_rows = rows_recv.at[pl.ds(0, n - 1)]
@@ -274,7 +276,6 @@
         lane < BENCH, 1.0 / token_total, EXPERTS / (TOP * token_total)
     )
     shared.wait_send()
-    mixed_cp.wait()
 
 
 def finish(mixed_in, sums_in, mixed_ref, load_ref, loss_ref):
@@ -298,11 +299,11 @@
     mixed, sums = pl.pallas_call(
         functools.partial(kernel, n, cap),
         out_shape=(
-            jax.ShapeDtypeStruct((rows, width), BF16),
-            jax.ShapeDtypeStruct((1, 128), F32),
+            pltpu.VMEM((rows, width), BF16),
+            pltpu.VMEM((1, 128), F32),
         ),
         in_specs=[hbm] * 8,
-        out_specs=(hbm, pl.BlockSpec(memory_space=pltpu.VMEM)),
+        out_specs=(pl.BlockSpec(memory_space=pltpu.VMEM), pl.BlockSpec(memory_space=pltpu.VMEM)),
         scratch_shapes=[
             pltpu.VMEM((rows, width), BF16),
             pltpu.VMEM((TOP, rows), I32),
@@ -311,23 +312,22 @@
             pltpu.VMEM((1, seqs), I32),
             pltpu.VMEM((rows, width), BF16),
             pltpu.VMEM((width, 2 * hid), BF16),
-            pltpu.VMEM((hid, width), BF16),
+            pltpu.VMEM((hid, half), BF16),
             pltpu.VMEM((2, EXPERTS, cap, half), BF16),
             pltpu.VMEM((2, n, cap, half), BF16),
-            pltpu.VMEM((pieces, n * cap, half // pieces), BF16),
-            pltpu.VMEM((pieces, n * cap, half // pieces), BF16),
+            pltpu.VMEM((hid, half), BF16),
+            pltpu.VMEM((n * cap, hid), BF16),
+            pltpu.VMEM((n * cap, hid), BF16),
             pltpu.VMEM((pieces, n, cap, half // pieces), BF16),
             pltpu.VMEM((2, pieces, n // 2, cap, half // pieces), BF16),
-            pltpu.VMEM((rows, width), BF16),
             pltpu.VMEM((1, 1, 128), F32),
             pltpu.VMEM((n, 1, 128), F32),
             pltpu.SemaphoreType.DMA((4,)),
             pltpu.SemaphoreType.DMA((2,)),
             pltpu.SemaphoreType.DMA((3,)),
             pltpu.SemaphoreType.DMA((4, pieces)),
-            pltpu.SemaphoreType.DMA((4,)),
-            pltpu.SemaphoreType.DMA((4,)),
-            pltpu.SemaphoreType.DMA,
+            pltpu.SemaphoreType.DMA((5,)),
+            pltpu.SemaphoreType.DMA((5,)),
         ],
         compiler_params=pltpu.CompilerParams(
             collective_id=0, has_side_effects=True, vmem_limit_bytes=60 * 1024 * 1024
@@ -352,7 +352,10 @@
         ),
         in_specs=[vmem, vmem],
         out_specs=(vmem, vmem, vmem),
-    )(mixed, sums)
+    )(
+        pltpu.with_memory_space_constraint(mixed, pltpu.VMEM),
+        pltpu.with_memory_space_constraint(sums, pltpu.VMEM),
+    )
     return mixed, load.reshape(EXPERTS), bench_loss.reshape(BENCH)
 
 

time: 27.1 us -> 25.8 us (0.952)
  Pallas kernels: 26.2 us -> 25 us
    pallas_call x1, Pallas kernels: 1.38 us -> 0.62 us  [on_device(): pl.pallas_call(finish, out_shape=(jax.ShapeDtypeStruct((rows, width), BF1...]
    pallas_call x1, Pallas kernels: 24.8 us -> 24.4 us  [on_device(): pl.pallas_call(functools.partial(kernel, n, cap), out_shape=(pltpu.VMEM((...]
where the time goes in v3:
time: 25.8 us; the launch traced here: 25.7 us
  Pallas kernels  25 us (97%)
  between operations  0.64 us (2%)
    pallas_call x1, Pallas kernels, on_device(): pl.pallas_call(functools.partial(kernel, n, cap), out_shape=(pltpu.VMEM((...  24.4 us
    pallas_call x1, Pallas kernels, on_device(): pl.pallas_call(finish, out_shape=(jax.ShapeDtypeStruct((rows, width), BF1...  0.62 us

profile of v3, /device:TPU:0, one launch (start us, length us, event | category | flops | bytes accessed | tf_op | source)
XLA Modules:
  0.0 25.7 jit_solution(6771119287728704960)
XLA Ops:
  0.6 24.4 %shard_map.103 = (bf16[4,4096]{1,0:T(4,128)(2,1)S(1)}, f32[1,128]{1,0:T(1,128)S(1)}) custom-call(bf16[4,4096]{1,0:T(4,128)(2,1)} %tok_hbm.1, s32[2,4]{1,0:T(2,128)} %bitcast.6, f32[1,4]{1,0:T(1,128)} %bitcast.7, s32[1,32]{1,0:T(1,128)} %bitcast.8, s32[1,32]{1,0:T(1,128)} %bitcast.9, bf16[4,4096]{1,0:T(4,128)(2,1)} %target_hbm.1, ...), custom_call_target="tpu_custom_call" | custom-call | tf_op jit(solution)/shard_map/pallas_call | solution.py:299
  25.1 0.6 %shard_map.104 = (bf16[4,4096]{1,0:T(4,128)(2,1)}, f32[1,8]{1,0:T(1,128)}, f32[1,8]{1,0:T(1,128)}) custom-call(bf16[4,4096]{1,0:T(4,128)(2,1)S(1)} %get-tuple-element.8.mixed_in, f32[1,128]{1,0:T(1,128)S(1)} %get-tuple-element.9.sums_in), custom_call_target="tpu_custom_call" | custom-call | tf_op jit(solution)/shard_map/pallas_call | solution.py:346
